TPU v7x, 32 devices: a whole 2x2x4 slice. The times are simulated.
32 devices in a mesh: rows: 4 (over x, core), seq: 8 (over z, y).
Axes of the slice: x: 2, y: 2, z: 4, core: 2. Of those that a mesh axis runs over, the one named last changes fastest.
Arguments:
- layer_in: bfloat16 [32, 1024, 768], P('rows', 'seq'), may hold values from -6 to 6
- cotangent: bfloat16 [32, 1024, 768], P('rows', 'seq'), may hold values from -6 to 6
- seg_lengths: int32 [32, 4], P('rows'), may hold values from 1 to 384, as said below
- query_weight: bfloat16 [768, 768], P(('rows', 'seq')), may hold values from -0.21875 to 0.21875
- query_bias: bfloat16 [768], P(('rows', 'seq')), may hold values from -3 to 3
- key_weight: bfloat16 [768, 768], P(('rows', 'seq')), may hold values from -0.21875 to 0.21875
- value_weight: bfloat16 [768, 768], P(('rows', 'seq')), may hold values from -0.21875 to 0.21875
- value_bias: bfloat16 [768], P(('rows', 'seq')), may hold values from -3 to 3
- out_weight: bfloat16 [768, 768], P(('rows', 'seq')), may hold values from -0.875 to 0.875
- out_bias: bfloat16 [768], P(('rows', 'seq')), may hold values from -2 to 2
- attn_gain: bfloat16 [768], P(('rows', 'seq')), may hold values from 0.5 to 1.5
- attn_shift: bfloat16 [768], P(('rows', 'seq')), may hold values from -2 to 2
- inner_weight: bfloat16 [768, 3072], P(('rows', 'seq')), may hold values from -0.21875 to 0.21875
- inner_bias: bfloat16 [3072], P(('rows', 'seq')), may hold values from -3 to 3
- outer_weight: bfloat16 [3072, 768], P(('rows', 'seq')), may hold values from -0.21875 to 0.21875
- outer_bias: bfloat16 [768], P(('rows', 'seq')), may hold values from -2 to 2
- final_gain: bfloat16 [768], P(('rows', 'seq')), may hold values from 0.5 to 1.5
- final_shift: bfloat16 [768], P(('rows', 'seq')), may hold values from -2 to 2
Outputs:
- layer_out: bfloat16 [32, 1024, 768], P('rows', 'seq')
- grad_in: float32 [32, 1024, 768], P('rows', 'seq')
- grad_query_weight: float32 [768, 768], P(('rows', 'seq'))
- grad_query_bias: float32 [768], P(('rows', 'seq'))
- grad_key_weight: float32 [768, 768], P(('rows', 'seq'))
- grad_value_weight: float32 [768, 768], P(('rows', 'seq'))
- grad_value_bias: float32 [768], P(('rows', 'seq'))
- grad_out_weight: float32 [768, 768], P(('rows', 'seq'))
- grad_out_bias: float32 [768], P(('rows', 'seq'))
- grad_attn_gain: float32 [768], P(('rows', 'seq'))
- grad_attn_shift: float32 [768], P(('rows', 'seq'))
- grad_inner_weight: float32 [768, 3072], P(('rows', 'seq'))
- grad_inner_bias: float32 [3072], P(('rows', 'seq'))
- grad_outer_weight: float32 [3072, 768], P(('rows', 'seq'))
- grad_outer_bias: float32 [768], P(('rows', 'seq'))
- grad_final_gain: float32 [768], P(('rows', 'seq'))
- grad_final_shift: float32 [768], P(('rows', 'seq'))
Inputs may be any that keep to these rules, and one draw needn't show every extreme that they name: `seg_lengths`: the lengths of each row sum to 960, and the positions past their sum are padding; the last segment of each row has exactly 384 tokens.
All inputs are finite; a program needn't handle non-finite values.
Results may differ from a plain program's by a relative error of at most 0.015.
Values may be sent and summed in bfloat16 or wider, within the bound.
A program may use at most 256 MiB of HBM per device.

v0:
```python
from functools import partial
import jax
import jax.numpy as jnp
from jax import lax
from jax.sharding import PartitionSpec as P

HEADS = 12
HEAD_DIM = 64
REACH = 3
epsilon = 1e-12
masked_score = -1e30


def passed_along(block, axis, distance):
    devices = range(lax.axis_size(axis))
    route = [(i - distance, i) for i in devices if i - distance in devices]
    return lax.ppermute(block, axis, route)


def segment_ids(lengths, positions, row_len):
    seg_ends = jnp.cumsum(lengths, axis=1)
    seg_count = jnp.sum(
        (positions[None, None, :] >= seg_ends[:, :, None]).astype(jnp.int32), axis=1
    )
    real_token = positions[None, :] < seg_ends[:, -1:]
    inside = (positions >= 0) & (positions < row_len)
    seg_id = jnp.where(real_token, seg_count, row_len + positions[None, :])
    return jnp.where(inside[None, :], seg_id, -1)


def norm_parts(values):
    row_mean = jnp.mean(values, axis=-1, keepdims=True)
    centred = values - row_mean
    inv_std = lax.rsqrt(jnp.mean(centred * centred, axis=-1, keepdims=True) + epsilon)
    return (centred * inv_std, inv_std)


def norm_back(upstream, normed, inv_std, gain_vec):
    scaled = upstream * gain_vec
    return inv_std * (
        scaled
        - jnp.mean(scaled, axis=-1, keepdims=True)
        - normed * jnp.mean(scaled * normed, axis=-1, keepdims=True)
    )


def split_window(window, features):
    key_rows = window[:, :features].reshape(window.shape[0], HEADS, HEAD_DIM)
    value_rows = window[:, features:].reshape(window.shape[0], HEADS, HEAD_DIM)
    return (key_rows, value_rows)


def row_scores(query_rows, key_rows, same_segment, score_scale):
    scores = (
        jnp.einsum("qhd,khd->hqk", query_rows, key_rows, preferred_element_type=jnp.float32)
        * score_scale
    )
    return jnp.where(same_segment[None], scores, masked_score)


def attend_row(pieces, score_scale):
    query_rows, window, same_segment = pieces
    key_rows, value_rows = split_window(window, query_rows.shape[1] * query_rows.shape[2])
    scores = row_scores(query_rows, key_rows, same_segment, score_scale)
    row_max = jnp.max(scores, axis=-1, keepdims=True)
    weights = jnp.exp(scores - row_max)
    row_total = jnp.sum(weights, axis=-1, keepdims=True)
    weights_b = (weights / row_total).astype(jnp.bfloat16)
    context = jnp.einsum("hqk,khd->qhd", weights_b, value_rows, preferred_element_type=jnp.float32)
    return (context.astype(jnp.bfloat16), (row_max + jnp.log(row_total))[..., 0])


def attend_back(pieces, score_scale):
    query_rows, window, same_segment, logsum, grad_context = pieces
    features = query_rows.shape[1] * query_rows.shape[2]
    key_rows, value_rows = split_window(window, features)
    scores = row_scores(query_rows, key_rows, same_segment, score_scale)
    probs = jnp.exp(scores - logsum[..., None])
    grad_probs = jnp.einsum(
        "qhd,khd->hqk", grad_context, value_rows, preferred_element_type=jnp.float32
    )
    grad_scores = (
        probs * (grad_probs - jnp.sum(grad_probs * probs, axis=-1, keepdims=True))
    ).astype(jnp.bfloat16)
    grad_query = (
        jnp.einsum("hqk,khd->qhd", grad_scores, key_rows, preferred_element_type=jnp.float32)
        * score_scale
    )
    grad_key = (
        jnp.einsum("hqk,qhd->khd", grad_scores, query_rows, preferred_element_type=jnp.float32)
        * score_scale
    )
    grad_value = jnp.einsum(
        "hqk,qhd->khd", probs.astype(jnp.bfloat16), grad_context, preferred_element_type=jnp.float32
    )
    width_keys = window.shape[0]
    return (
        grad_query,
        jnp.concatenate(
            [grad_key.reshape(width_keys, features), grad_value.reshape(width_keys, features)],
            axis=1,
        ),
    )


def near_distances():
    return list(range(REACH, 0, -1)) + list(range(-1, -REACH - 1, -1))


def near_window(kv_local):
    lower_side = []
    upper_side = []
    for distance in near_distances():
        arrived = passed_along(kv_local, "seq", distance)
        if distance > 0:
            lower_side.append(arrived)
        else:
            upper_side.append(arrived)
    return jnp.concatenate(lower_side + [kv_local] + upper_side, axis=1)


def near_back(grad_window, block_len):
    own_grad = grad_window[:, REACH * block_len : (REACH + 1) * block_len]
    for position in range(2 * REACH + 1):
        offset = position - REACH
        if offset != 0:
            grad_piece = grad_window[:, position * block_len : (position + 1) * block_len]
            own_grad = own_grad + passed_along(
                grad_piece.astype(jnp.bfloat16), "seq", offset
            ).astype(grad_piece.dtype)
    return own_grad


def body(
    layer_in,
    cotangent,
    seg_lengths,
    query_weight,
    query_bias,
    key_weight,
    value_weight,
    value_bias,
    out_weight,
    out_bias,
    attn_gain,
    attn_shift,
    inner_weight,
    inner_bias,
    outer_weight,
    outer_bias,
    final_gain,
    final_shift,
):
    shards = (
        query_weight,
        query_bias,
        key_weight,
        value_weight,
        value_bias,
        out_weight,
        out_bias,
        attn_gain,
        attn_shift,
        inner_weight,
        inner_bias,
        outer_weight,
        outer_bias,
        final_gain,
        final_shift,
    )
    gathered = (
        lax.all_gather(shards[0], ("rows", "seq"), axis=0, tiled=True),
        lax.all_gather(shards[1], ("rows", "seq"), axis=0, tiled=True),
        lax.all_gather(shards[2], ("rows", "seq"), axis=0, tiled=True),
        lax.all_gather(shards[3], ("rows", "seq"), axis=0, tiled=True),
        lax.all_gather(shards[4], ("rows", "seq"), axis=0, tiled=True),
        lax.all_gather(shards[5], ("rows", "seq"), axis=0, tiled=True),
        lax.all_gather(shards[6], ("rows", "seq"), axis=0, tiled=True),
        lax.all_gather(shards[7], ("rows", "seq"), axis=0, tiled=True),
        lax.all_gather(shards[8], ("rows", "seq"), axis=0, tiled=True),
        lax.all_gather(shards[9], ("rows", "seq"), axis=0, tiled=True),
        lax.all_gather(shards[10], ("rows", "seq"), axis=0, tiled=True),
        lax.all_gather(shards[11], ("rows", "seq"), axis=0, tiled=True),
        lax.all_gather(shards[12], ("rows", "seq"), axis=0, tiled=True),
        lax.all_gather(shards[13], ("rows", "seq"), axis=0, tiled=True),
        lax.all_gather(shards[14], ("rows", "seq"), axis=0, tiled=True),
    )
    (
        query_mat,
        query_vec,
        key_mat,
        value_mat,
        value_vec,
        out_mat,
        out_vec,
        attn_gain_f,
        attn_shift_f,
        inner_mat,
        inner_vec,
        outer_mat,
        outer_vec,
        final_gain_f,
        final_shift_f,
    ) = gathered
    row_count, block_len, features = layer_in.shape
    tokens = row_count * block_len
    score_scale = HEAD_DIM ** (-0.5)
    inputs = layer_in.reshape(tokens, features)
    query_flat = jnp.dot(inputs, query_mat, preferred_element_type=jnp.float32) + query_vec.astype(
        jnp.float32
    )
    query_b = query_flat.astype(jnp.bfloat16).reshape(row_count, block_len, HEADS, HEAD_DIM)
    kv_mat = jnp.concatenate([key_mat, value_mat], axis=1)
    kv_bias = jnp.concatenate([jnp.zeros_like(value_vec), value_vec]).astype(jnp.float32)
    kv_local = (
        (jnp.dot(inputs, kv_mat, preferred_element_type=jnp.float32) + kv_bias)
        .astype(jnp.bfloat16)
        .reshape(row_count, block_len, 2 * features)
    )
    seq_index = lax.axis_index("seq")
    row_len = block_len * lax.axis_size("seq")
    local_pos = seq_index * block_len + jnp.arange(block_len, dtype=jnp.int32)
    window_pos = (seq_index - REACH) * block_len + jnp.arange(
        (2 * REACH + 1) * block_len, dtype=jnp.int32
    )
    query_ids = segment_ids(seg_lengths, local_pos, row_len)
    key_ids = segment_ids(seg_lengths, window_pos, row_len)
    same_segment = query_ids[:, :, None] == key_ids[:, None, :]
    window = near_window(kv_local)
    context, logsum = lax.map(
        partial(attend_row, score_scale=score_scale), (query_b, window, same_segment)
    )
    context_flat = context.reshape(tokens, features)
    attended = jnp.dot(context_flat, out_mat, preferred_element_type=jnp.float32) + out_vec.astype(
        jnp.float32
    )
    first_sum = inputs.astype(jnp.float32) + attended
    normed_one, inv_std_one = norm_parts(first_sum)
    hidden = normed_one * attn_gain_f.astype(jnp.float32) + attn_shift_f.astype(jnp.float32)
    hidden_b = hidden.astype(jnp.bfloat16)
    inner_pre = jnp.dot(hidden_b, inner_mat, preferred_element_type=jnp.float32) + inner_vec.astype(
        jnp.float32
    )
    active, gelu_back = jax.vjp(partial(jax.nn.gelu, approximate=False), inner_pre)
    active_b = active.astype(jnp.bfloat16)
    outer_out = jnp.dot(active_b, outer_mat, preferred_element_type=jnp.float32) + outer_vec.astype(
        jnp.float32
    )
    normed_two, inv_std_two = norm_parts(hidden + outer_out)
    layer_out = (
        normed_two * final_gain_f.astype(jnp.float32) + final_shift_f.astype(jnp.float32)
    ).astype(jnp.bfloat16)
    real_token = (local_pos[None, :] < jnp.sum(seg_lengths, axis=1)[:, None]).astype(jnp.float32)
    upstream = (cotangent.astype(jnp.float32) * real_token[:, :, None]).reshape(tokens, features)
    grad_final_gain = jnp.sum(upstream * normed_two, axis=0)
    grad_final_shift = jnp.sum(upstream, axis=0)
    grad_second = norm_back(upstream, normed_two, inv_std_two, final_gain_f.astype(jnp.float32))
    grad_outer = grad_second.astype(jnp.bfloat16)
    grad_outer_bias = jnp.sum(grad_outer.astype(jnp.float32), axis=0)
    grad_outer_weight = jnp.einsum(
        "tf,td->fd", active_b, grad_outer, preferred_element_type=jnp.float32
    )
    grad_active = jnp.einsum("td,fd->tf", grad_outer, outer_mat, preferred_element_type=jnp.float32)
    grad_inner = gelu_back(grad_active)[0].astype(jnp.bfloat16)
    grad_inner_bias = jnp.sum(grad_inner.astype(jnp.float32), axis=0)
    grad_inner_weight = jnp.einsum(
        "td,tf->df", hidden_b, grad_inner, preferred_element_type=jnp.float32
    )
    grad_hidden = grad_second + jnp.einsum(
        "tf,df->td", grad_inner, inner_mat, preferred_element_type=jnp.float32
    )
    grad_attn_gain = jnp.sum(grad_hidden * normed_one, axis=0)
    grad_attn_shift = jnp.sum(grad_hidden, axis=0)
    grad_first = norm_back(grad_hidden, normed_one, inv_std_one, attn_gain_f.astype(jnp.float32))
    grad_attended = grad_first.astype(jnp.bfloat16)
    grad_out_bias = jnp.sum(grad_attended.astype(jnp.float32), axis=0)
    grad_out_weight = jnp.einsum(
        "td,te->de", context_flat, grad_attended, preferred_element_type=jnp.float32
    )
    grad_context = jnp.einsum(
        "te,de->td", grad_attended, out_mat, preferred_element_type=jnp.float32
    ).astype(jnp.bfloat16)
    grad_context = grad_context.reshape(row_count, block_len, HEADS, HEAD_DIM)
    grad_query, grad_window = lax.map(
        partial(attend_back, score_scale=score_scale),
        (query_b, window, same_segment, logsum, grad_context),
    )
    grad_kv = near_back(grad_window, block_len)
    grad_query_b = grad_query.reshape(tokens, features).astype(jnp.bfloat16)
    grad_kv_b = grad_kv.reshape(tokens, 2 * features).astype(jnp.bfloat16)
    grad_query_weight = jnp.einsum(
        "td,te->de", inputs, grad_query_b, preferred_element_type=jnp.float32
    )
    grad_query_bias = jnp.sum(grad_query_b.astype(jnp.float32), axis=0)
    grad_kv_weight = jnp.einsum("td,te->de", inputs, grad_kv_b, preferred_element_type=jnp.float32)
    grad_value_bias = jnp.sum(grad_kv_b[:, features:].astype(jnp.float32), axis=0)
    grad_in = grad_first + jnp.einsum(
        "te,de->td", grad_query_b, query_mat, preferred_element_type=jnp.float32
    )
    grad_in = grad_in + jnp.einsum(
        "te,de->td", grad_kv_b, kv_mat, preferred_element_type=jnp.float32
    )
    partial_grads = (
        grad_query_weight,
        grad_query_bias,
        grad_kv_weight[:, :features],
        grad_kv_weight[:, features:],
        grad_value_bias,
        grad_out_weight,
        grad_out_bias,
        grad_attn_gain,
        grad_attn_shift,
        grad_inner_weight,
        grad_inner_bias,
        grad_outer_weight,
        grad_outer_bias,
        grad_final_gain,
        grad_final_shift,
    )
    owned = (
        lax.psum_scatter(partial_grads[0], ("rows", "seq"), scatter_dimension=0, tiled=True),
        lax.psum_scatter(partial_grads[1], ("rows", "seq"), scatter_dimension=0, tiled=True),
        lax.psum_scatter(partial_grads[2], ("rows", "seq"), scatter_dimension=0, tiled=True),
        lax.psum_scatter(partial_grads[3], ("rows", "seq"), scatter_dimension=0, tiled=True),
        lax.psum_scatter(partial_grads[4], ("rows", "seq"), scatter_dimension=0, tiled=True),
        lax.psum_scatter(partial_grads[5], ("rows", "seq"), scatter_dimension=0, tiled=True),
        lax.psum_scatter(partial_grads[6], ("rows", "seq"), scatter_dimension=0, tiled=True),
        lax.psum_scatter(partial_grads[7], ("rows", "seq"), scatter_dimension=0, tiled=True),
        lax.psum_scatter(partial_grads[8], ("rows", "seq"), scatter_dimension=0, tiled=True),
        lax.psum_scatter(partial_grads[9], ("rows", "seq"), scatter_dimension=0, tiled=True),
        lax.psum_scatter(partial_grads[10], ("rows", "seq"), scatter_dimension=0, tiled=True),
        lax.psum_scatter(partial_grads[11], ("rows", "seq"), scatter_dimension=0, tiled=True),
        lax.psum_scatter(partial_grads[12], ("rows", "seq"), scatter_dimension=0, tiled=True),
        lax.psum_scatter(partial_grads[13], ("rows", "seq"), scatter_dimension=0, tiled=True),
        lax.psum_scatter(partial_grads[14], ("rows", "seq"), scatter_dimension=0, tiled=True),
    )
    g_qw, g_qb, g_kw, g_vw, g_vb, g_ow, g_ob, g_ag, g_as, g_iw, g_ib, g_tw, g_tb, g_fg, g_fs = owned
    return (
        layer_out.reshape(row_count, block_len, features),
        grad_in.reshape(row_count, block_len, features),
        g_qw,
        g_qb,
        g_kw,
        g_vw,
        g_vb,
        g_ow,
        g_ob,
        g_ag,
        g_as,
        g_iw,
        g_ib,
        g_tw,
        g_tb,
        g_fg,
        g_fs,
    )


def solution(mesh):
    placed = (
        P("rows", "seq", None),
        P("rows", "seq", None),
        P("rows", None),
        P(("rows", "seq"), None),
        P(("rows", "seq")),
        P(("rows", "seq"), None),
        P(("rows", "seq"), None),
        P(("rows", "seq")),
        P(("rows", "seq"), None),
        P(("rows", "seq")),
        P(("rows", "seq")),
        P(("rows", "seq")),
        P(("rows", "seq"), None),
        P(("rows", "seq")),
        P(("rows", "seq"), None),
        P(("rows", "seq")),
        P(("rows", "seq")),
        P(("rows", "seq")),
    )
    return jax.shard_map(
        body,
        mesh=mesh,
        in_specs=placed,
        out_specs=(
            P("rows", "seq", None),
            P("rows", "seq", None),
            P(("rows", "seq"), None),
            P(("rows", "seq")),
            P(("rows", "seq"), None),
            P(("rows", "seq"), None),
            P(("rows", "seq")),
            P(("rows", "seq"), None),
            P(("rows", "seq")),
            P(("rows", "seq")),
            P(("rows", "seq")),
            P(("rows", "seq"), None),
            P(("rows", "seq")),
            P(("rows", "seq"), None),
            P(("rows", "seq")),
            P(("rows", "seq")),
            P(("rows", "seq")),
        ),
        check_vma=False,
    )
```

profile of v0, /device:TPU:0, one launch (start us, length us, event | category | flops | bytes accessed | tf_op | source)
XLA Modules:
  0.0 1829.5 jit_solution(7902769398490669864)
XLA Ops:
  18.2 42.3 %all-reduce.20 = (bf16[768]{0:T(1024)(128)(2,1)S(1)}, bf16[768]{0:T(1024)(128)(2,1)S(1)}, bf16[768]{0:T(1024)(128)(2,1)S(1)}, bf16[768]{0:T(1024)(128)(2,1)S(1)}...) all-reduce(bf16[768]{0:T(1024)(128)(2,1)S(1)} %dynamic-update-slice, ...), channel_id=1, replica_groups=mesh['rows'=4,'seq'=8] {'rows','seq'}, use_global_device_ids=true, to_apply=%add.3 | all-reduce | flops 9216 | bytes 36864
  60.5 7.4 all-gather.7.cloned.1.call-done
  69.2 54.8 %all-gather.9.cloned.1.call-done = bf16[768,768]{1,0:T(8,128)(2,1)} async-done(((bf16[24,768]{1,0:T(8,128)(2,1)}), bf16[768,768]{1,0:T(8,128)(2,1)}) %all-gather.9.cloned.1.call-update) | async-done | bytes 1179664 | tf_op jit(solution)/shard_map/all_gather | solution.py:175
  142.7 5.1 collective-permute-start.2
  155.5 104.2 %collective-permute-done = bf16[8,128,1536]{1,2,0:T(8,128)(2,1)S(1)} collective-permute-done((bf16[8,128,1536]{1,2,0:T(8,128)(2,1)}, bf16[8,128,1536]{1,2,0:T(8,128)(2,1)S(1)}, u32[]{:S(2)}, u32[]{:S(2)}) %collective-permute-start) | collective-permute-done | bytes 3145760 | tf_op jit(solution)/shard_map/ppermute | solution.py:17
  263.5 147.9 %all-gather.11.cloned.1.call-done = bf16[768,768]{1,0:T(8,128)(2,1)} async-done(((bf16[24,768]{1,0:T(8,128)(2,1)}), bf16[768,768]{1,0:T(8,128)(2,1)}) %all-gather.11.cloned.1.call-update) | async-done | bytes 1179664 | tf_op jit(solution)/shard_map/all_gather | solution.py:172
  435.9 7.3 copy-done
  443.2 64.7 %while.24 = (s32[]{:T(128)}, bf16[8,128,12,64]{1,3,2,0:T(8,128)(2,1)}, f32[8,12,128]{2,1,0:T(8,128)}, bf16[8,896,1536]{1,2,0:T(8,128)(2,1)}, pred[8,128,896]{2,1...) while((s32[]{:T(128)}, bf16[8,128,12,64]{1,3,2,0:T(8,128)(2,1)}, ...), condition=%wide.region_6.7_spmd, body=%wide.region_3.6_spmd.sunk | while | flops 368933376 | bytes 31295592 | solution.py:230
  518.9 60.8 %all-gather.15.cloned.1.call-done = bf16[768,3072]{1,0:T(8,128)(2,1)} async-done(((bf16[24,3072]{1,0:T(8,128)(2,1)}), bf16[768,3072]{1,0:T(8,128)(2,1)}) %all-gather.15.cloned.1.call-update) | async-done | bytes 4718608 | tf_op jit(solution)/shard_map/all_gather | solution.py:181
  579.7 35.8 %multiply_convert_fusion.1 = (bf16[1024,3072]{1,0:T(8,128)(2,1)}, f32[1024,3072]{1,0:T(8,128)}, f32[1024,3072]{1,0:T(8,128)}) fusion(f32[3072]{0:T(1024)S(1)} %convert_element_type.160, bf16[768,3072]{1,0:T(8,128)(2,1)} %all-gather.15.cloned.1.call-done, f32[1024,768]{1,0:T(8,128)S(1)} %get-tuple-element.300, f32[768]{0:T(1024)S(1)} %convert_element_type.158, ...), kind=kOutput, calls=%fused_computation.56 | convolution fusion | flops 5043388416 | bytes 39348224 | tf_op jit(solution)/shard_map/dot_general | solution.py:241
  615.5 28.9 %all-gather.17.cloned.1.call-done = bf16[3072,768]{1,0:T(8,128)(2,1)} async-done(((bf16[96,768]{1,0:T(8,128)(2,1)}), bf16[3072,768]{1,0:T(8,128)(2,1)}) %all-gather.17.cloned.1.call-update) | async-done | bytes 4718608 | tf_op jit(solution)/shard_map/all_gather | solution.py:183
  644.3 8.8 fusion.75
  660.4 19.5 %convert_reduce_fusion = (f32[3072]{0:T(1024)}, bf16[1024,3072]{1,0:T(8,128)(2,1)}) fusion(f32[1024,3072]{1,0:T(8,128)} %get-tuple-element.280, bf16[3072,768]{1,0:T(8,128)(2,1)} %all-gather.17.cloned.1.call-done, f32[1024,768]{1,0:T(8,128)} %get-tuple-element.276, f32[1024,3072]{1,0:T(8,128)} %get-tuple-element.301, f32[3072]{0:T(1024)S(1)} %convert_element_type.160), kind=kOutput, calls=%fused_computation.54 | convolution fusion | flops 4886098944 | bytes 39346176 | tf_op jit(solution)/shard_map/td,fd->tf/dot_general | solution.py:263
  679.9 10.6 multiply_reduce_fusion.1
  697.6 225.8 %while.25 = (s32[]{:T(128)}, bf16[8,128,12,64]{1,3,2,0:T(8,128)(2,1)S(1)}, f32[8,896,1536]{2,1,0:T(8,128)}, bf16[8,896,1536]{1,2,0:T(8,128)(2,1)}, pred[8,128,89...) while((s32[]{:T(128)}, ...), condition=%wide.region_18.19_spmd, body=%wide.region_16.18_spmd.sunk | while | flops 903608832 | bytes 96761984 | solution.py:284
  714.7 6.1 copy.163
  720.8 5.3 constant_dynamic-update-slice_fusion.11
  742.8 6.1 copy.163
  749.0 5.4 constant_dynamic-update-slice_fusion.11
  771.0 6.1 copy.163
  777.2 5.3 constant_dynamic-update-slice_fusion.11
  799.2 6.1 copy.163
  805.3 5.3 constant_dynamic-update-slice_fusion.11
  827.3 6.1 copy.163
  833.5 5.4 constant_dynamic-update-slice_fusion.11
  855.5 6.1 copy.163
  861.7 5.3 constant_dynamic-update-slice_fusion.11
  883.6 6.1 copy.163
  889.8 5.4 constant_dynamic-update-slice_fusion.11
  911.9 6.1 copy.163
  918.0 5.3 constant_dynamic-update-slice_fusion.11
  923.4 23.9 %convert.8 = bf16[8,896,1536]{2,1,0:T(8,128)(2,1)} convert(f32[8,896,1536]{2,1,0:T(8,128)} %get-tuple-element.96) | non-fusion elementwise | flops 11010048 | bytes 66060288 | tf_op jit(solution)/shard_map/convert.5
  947.3 13.6 fusion.72
  965.0 7.1 collective-permute-start.11
  972.1 6.6 collective-permute-start.10
  984.4 52.0 %collective-permute-done.6 = bf16[8,128,1536]{2,1,0:T(8,128)(2,1)} collective-permute-done((bf16[8,128,1536]{2,1,0:T(8,128)(2,1)}, bf16[8,128,1536]{2,1,0:T(8,128)(2,1)}, u32[]{:S(2)}, u32[]{:S(2)}) %collective-permute-start.6) | collective-permute-done | bytes 3145760 | tf_op jit(solution)/shard_map/ppermute | solution.py:17
  1045.1 57.5 %collective-permute-done.11 = bf16[8,128,1536]{2,1,0:T(8,128)(2,1)} collective-permute-done((bf16[8,128,1536]{2,1,0:T(8,128)(2,1)}, bf16[8,128,1536]{2,1,0:T(8,128)(2,1)}, u32[]{:S(2)}, u32[]{:S(2)}) %collective-permute-start.11) | collective-permute-done | bytes 3145760 | tf_op jit(solution)/shard_map/ppermute | solution.py:17
  1102.6 68.6 %collective-permute-done.10 = bf16[8,128,1536]{2,1,0:T(8,128)(2,1)} collective-permute-done((bf16[8,128,1536]{2,1,0:T(8,128)(2,1)}, bf16[8,128,1536]{2,1,0:T(8,128)(2,1)}, u32[]{:S(2)}, u32[]{:S(2)}) %collective-permute-start.10) | collective-permute-done | bytes 3145760 | tf_op jit(solution)/shard_map/ppermute | solution.py:17
  1171.1 11.7 collective-permute-done.9
  1187.6 9.9 add_convert_fusion.1
  1207.4 10.7 fusion.65
  1220.0 10.2 fusion.62
  1237.4 107.5 %all-reduce.19 = (f32[768]{0:T(1024)S(1)}, f32[768]{0:T(1024)S(1)}, f32[768]{0:T(1024)S(1)}, f32[768]{0:T(1024)S(1)}, f32[768]{0:T(1024)S(1)}, /*index=5*/f32[30...) all-reduce(f32[768]{0:T(1024)S(1)} %reduce_sum.212, ...), channel_id=3, replica_groups=mesh['rows'=4,'seq'=8] {'rows','seq'}, use_global_device_ids=true, to_apply=%region_21.22.clone | all-reduce | flops 9216 | bytes 73728
  1350.2 6.7 add_add_fusion
  1356.9 78.0 %reduce-scatter.23.cloned.1.call-done = f32[24,768]{1,0:T(8,128)} async-done(((f32[768,768]{1,0:T(8,128)}), f32[24,768]{1,0:T(8,128)}) %reduce-scatter.23.cloned.1.call-update) | async-done | bytes 73744
  1434.9 104.3 %reduce-scatter.21.cloned.1.call-done = f32[24,768]{1,0:T(8,128)} async-done(((f32[768,768]{1,0:T(8,128)}), f32[24,768]{1,0:T(8,128)}) %reduce-scatter.21.cloned.1.call-update) | async-done | bytes 73744
  1539.2 141.7 %reduce-scatter.15.cloned.1.call-done = f32[24,3072]{1,0:T(8,128)} async-done(((f32[768,3072]{1,0:T(8,128)}), f32[24,3072]{1,0:T(8,128)}) %reduce-scatter.15.cloned.1.call-update) | async-done | bytes 294928 | tf_op jit(solution)/shard_map/reduce_scatter | solution.py:330
  1680.9 141.5 %reduce-scatter.17.cloned.1.call-done = f32[96,768]{1,0:T(8,128)} async-done(((f32[3072,768]{1,0:T(8,128)}), f32[96,768]{1,0:T(8,128)}) %reduce-scatter.17.cloned.1.call-update) | async-done | bytes 294928 | tf_op jit(solution)/shard_map/reduce_scatter | solution.py:332
  (371 shorter events, 336.3 us)
Async XLA Ops:
  7.2 60.7 %all-gather.7.cloned.1.call-start = ((), (), s32[]{:S(2)}) async-start(), calls=%async_computation.6 | async-start | bytes 1216512 | tf_op jit(solution)/shard_map/all_gather | solution.py:174
  7.9 116.1 %all-gather.9.cloned.1.call-start = ((), (), s32[]{:S(2)}) async-start(), calls=%async_computation.7 | async-start | bytes 1216512 | tf_op jit(solution)/shard_map/all_gather | solution.py:175
  8.7 402.8 %all-gather.11.cloned.1.call-start = ((), (), s32[]{:S(2)}) async-start(), calls=%async_computation.8 | async-start | bytes 1216512 | tf_op jit(solution)/shard_map/all_gather | solution.py:172
  9.4 505.1 %all-gather.13.cloned.1.call-start = ((), (), s32[]{:S(2)}) async-start(), calls=%async_computation.9 | async-start | bytes 1216512 | tf_op jit(solution)/shard_map/all_gather | solution.py:177
  10.0 569.7 %all-gather.15.cloned.1.call-start = ((), (), s32[]{:S(2)}) async-start(), calls=%async_computation.10 | async-start | bytes 4866048 | tf_op jit(solution)/shard_map/all_gather | solution.py:181
  10.6 633.8 %all-gather.17.cloned.1.call-start = ((), (), s32[]{:S(2)}) async-start(), calls=%async_computation.11 | async-start | bytes 4866048 | tf_op jit(solution)/shard_map/all_gather | solution.py:183
  131.5 6.5 copy-start.36
  134.4 125.3 %collective-permute-start = (bf16[8,128,1536]{1,2,0:T(8,128)(2,1)}, bf16[8,128,1536]{1,2,0:T(8,128)(2,1)S(1)}, u32[]{:S(2)}, u32[]{:S(2)}) collective-permute-start(bf16[8,128,1536]{1,2,0:T(8,128)(2,1)} %copy.94), channel_id=1, source_target_pairs={{0,3},{1,4},{2,5},{3,6},{4,7},{8,11},{9,12},{10,13},{11,14},{12,15... | collective-permute-start | bytes 9437192 | tf_op jit(solution)/shard_map/ppermute | solution.py:17
  138.0 1218.9 %reduce-scatter.13.cloned.1.call-start = ((), (), s32[]{:S(2)}) async-start(), calls=%async_computation.12 | async-start | bytes 2433024 | tf_op jit(solution)/shard_map/reduce_scatter | solution.py:326
  138.1 281.8 %collective-permute-start.1 = (bf16[8,128,1536]{1,2,0:T(8,128)(2,1)}, bf16[8,128,1536]{1,2,0:T(8,128)(2,1)}, u32[]{:S(2)}, u32[]{:S(2)}) collective-permute-start(bf16[8,128,1536]{1,2,0:T(8,128)(2,1)} %copy.94), channel_id=1, source_target_pairs={{0,2},{1,3},{2,4},{3,5},{4,6},{5,7},{8,10},{9,11},{10,12},{11,13},... | collective-permute-start | bytes 9437192 | tf_op jit(solution)/shard_map/ppermute | solution.py:17
  142.7 279.8 %collective-permute-start.2 = (bf16[8,128,1536]{1,2,0:T(8,128)(2,1)}, bf16[8,128,1536]{1,2,0:T(8,128)(2,1)}, u32[]{:S(2)}, u32[]{:S(2)}) collective-permute-start(bf16[8,128,1536]{1,2,0:T(8,128)(2,1)} %copy.94), channel_id=1, source_target_pairs={{0,1},{1,2},{2,3},{3,4},{4,5},{5,6},{6,7},{8,9},{9,10},{10,11},{11... | collective-permute-start | bytes 9437192 | tf_op jit(solution)/shard_map/ppermute | solution.py:17
  147.9 111.8 %copy-start.27 = (f32[768]{0:T(1024)}, f32[768]{0:T(1024)S(1)}, u32[]{:S(2)}) copy-start(f32[768]{0:T(1024)S(1)} %convert_element_type.163) | copy-start | bytes 9220
  152.2 275.7 %collective-permute-start.3 = (bf16[8,128,1536]{1,2,0:T(8,128)(2,1)}, bf16[8,128,1536]{1,2,0:T(8,128)(2,1)}, u32[]{:S(2)}, u32[]{:S(2)}) collective-permute-start(bf16[8,128,1536]{1,2,0:T(8,128)(2,1)} %copy.94), channel_id=1, source_target_pairs={{1,0},{2,1},{3,2},{4,3},{5,4},{6,5},{7,6},{9,8},{10,9},{11,10},{12... | collective-permute-start | bytes 9437192 | tf_op jit(solution)/shard_map/ppermute | solution.py:17
  153.6 277.0 %collective-permute-start.4 = (bf16[8,128,1536]{1,2,0:T(8,128)(2,1)}, bf16[8,128,1536]{1,2,0:T(8,128)(2,1)}, u32[]{:S(2)}, u32[]{:S(2)}) collective-permute-start(bf16[8,128,1536]{1,2,0:T(8,128)(2,1)} %copy.94), channel_id=1, source_target_pairs={{2,0},{3,1},{4,2},{5,3},{6,4},{7,5},{10,8},{11,9},{12,10},{13,11},... | collective-permute-start | bytes 9437192 | tf_op jit(solution)/shard_map/ppermute | solution.py:17
  259.7 173.6 %collective-permute-start.5 = (bf16[8,128,1536]{1,2,0:T(8,128)(2,1)}, bf16[8,128,1536]{1,2,0:T(8,128)(2,1)}, u32[]{:S(2)}, u32[]{:S(2)}) collective-permute-start(bf16[8,128,1536]{1,2,0:T(8,128)(2,1)} %copy.94), channel_id=1, source_target_pairs={{3,0},{4,1},{5,2},{6,3},{7,4},{11,8},{12,9},{13,10},{14,11},{15,12... | collective-permute-start | bytes 9437192 | tf_op jit(solution)/shard_map/ppermute | solution.py:17
  261.5 429.0 %copy-start.23 = (f32[768]{0:T(1024)}, f32[768]{0:T(1024)S(1)}, u32[]{:S(2)}) copy-start(f32[768]{0:T(1024)S(1)} %convert_element_type.157) | copy-start | bytes 9220
  261.5 382.8 %copy-start.25 = (f32[768]{0:T(1024)}, f32[768]{0:T(1024)S(1)}, u32[]{:S(2)}) copy-start(f32[768]{0:T(1024)S(1)} %convert_element_type.158) | copy-start | bytes 9220
  435.9 7.3 copy-start
  507.9 6.6 copy-start.4
  507.9 6.6 copy-start.10
  518.4 172.1 %copy-start.1 = (f32[1024,768]{1,0:T(8,128)}, f32[1024,768]{1,0:T(8,128)S(1)}, u32[]{:S(2)}) copy-start(f32[1024,768]{1,0:T(8,128)S(1)} %get-tuple-element.300) | copy-start | bytes 9437188
  518.4 172.1 %copy-start.19 = (f32[1024]{0:T(1024)}, f32[1024]{0:T(1024)S(1)}, u32[]{:S(2)}) copy-start(f32[1024]{0:T(1024)S(1)} %broadcast_multiply_fusion.4) | copy-start | bytes 12292
  518.9 171.6 %copy-start.21 = (f32[1024]{0:T(1024)}, f32[1024]{0:T(1024)S(1)}, u32[]{:S(2)}) copy-start(f32[1024]{0:T(1024)S(1)} %add_rsqrt_fusion.1) | copy-start | bytes 12292
  518.9 125.4 %copy-start.37 = (f32[768]{0:T(1024)S(1)}, f32[768]{0:T(1024)}, u32[]{:S(2)}) copy-start(f32[768]{0:T(1024)} %convert_element_type.162) | copy-start | bytes 9220
  690.5 3.5 copy-start.41
  923.4 114.5 %copy-start.8 = (bf16[8,128,12,64]{1,3,2,0:T(8,128)(2,1)}, bf16[8,128,12,64]{1,3,2,0:T(8,128)(2,1)S(1)}, u32[]{:S(2)}) copy-start(bf16[8,128,12,64]{1,3,2,0:T(8,128)(2,1)S(1)} %get-tuple-element.95) | copy-start | bytes 4718596
  947.3 14.9 copy-start.14
  947.3 14.9 copy-start.16
  960.9 75.5 %collective-permute-start.6 = (bf16[8,128,1536]{2,1,0:T(8,128)(2,1)}, bf16[8,128,1536]{2,1,0:T(8,128)(2,1)}, u32[]{:S(2)}, u32[]{:S(2)}) collective-permute-start(bf16[8,128,1536]{2,1,0:T(8,128)(2,1)} %get-tuple-element.289), channel_id=1, source_target_pairs={{3,0},{4,1},{5,2},{6,3},{7,4},{11,8},{12,9},{13,10},{14,11},{15,12... | collective-permute-start | bytes 9437192 | tf_op jit(solution)/shard_map/ppermute | solution.py:17
  965.0 391.9 %reduce-scatter.19.cloned.1.call-start = ((), (), s32[]{:S(2)}) async-start(), calls=%async_computation.15 | async-start | bytes 2433024
  965.0 137.6 %collective-permute-start.11 = (bf16[8,128,1536]{2,1,0:T(8,128)(2,1)}, bf16[8,128,1536]{2,1,0:T(8,128)(2,1)}, u32[]{:S(2)}, u32[]{:S(2)}) collective-permute-start(bf16[8,128,1536]{2,1,0:T(8,128)(2,1)} %get-tuple-element.290), channel_id=1, source_target_pairs={{0,3},{1,4},{2,5},{3,6},{4,7},{8,11},{9,12},{10,13},{11,14},{12,15... | collective-permute-start | bytes 9437192 | tf_op jit(solution)/shard_map/ppermute | solution.py:17
  972.1 199.0 %collective-permute-start.10 = (bf16[8,128,1536]{2,1,0:T(8,128)(2,1)}, bf16[8,128,1536]{2,1,0:T(8,128)(2,1)}, u32[]{:S(2)}, u32[]{:S(2)}) collective-permute-start(bf16[8,128,1536]{2,1,0:T(8,128)(2,1)} %get-tuple-element.291), channel_id=1, source_target_pairs={{0,2},{1,3},{2,4},{3,5},{4,6},{5,7},{8,10},{9,11},{10,12},{11,13},... | collective-permute-start | bytes 9437192 | tf_op jit(solution)/shard_map/ppermute | solution.py:17
  978.7 204.1 %collective-permute-start.9 = (bf16[8,128,1536]{2,1,0:T(8,128)(2,1)}, bf16[8,128,1536]{2,1,0:T(8,128)(2,1)}, u32[]{:S(2)}, u32[]{:S(2)}) collective-permute-start(bf16[8,128,1536]{2,1,0:T(8,128)(2,1)} %get-tuple-element.292), channel_id=1, source_target_pairs={{0,1},{1,2},{2,3},{3,4},{4,5},{5,6},{6,7},{8,9},{9,10},{10,11},{11... | collective-permute-start | bytes 9437192 | tf_op jit(solution)/shard_map/ppermute | solution.py:17
  983.1 199.7 %collective-permute-start.8 = (bf16[8,128,1536]{2,1,0:T(8,128)(2,1)}, bf16[8,128,1536]{2,1,0:T(8,128)(2,1)}, u32[]{:S(2)}, u32[]{:S(2)}) collective-permute-start(bf16[8,128,1536]{2,1,0:T(8,128)(2,1)} %get-tuple-element.293), channel_id=1, source_target_pairs={{1,0},{2,1},{3,2},{4,3},{5,4},{6,5},{7,6},{9,8},{10,9},{11,10},{12... | collective-permute-start | bytes 9437192 | tf_op jit(solution)/shard_map/ppermute | solution.py:17
  1036.4 151.2 %collective-permute-start.7 = (bf16[8,128,1536]{2,1,0:T(8,128)(2,1)}, bf16[8,128,1536]{2,1,0:T(8,128)(2,1)}, u32[]{:S(2)}, u32[]{:S(2)}) collective-permute-start(bf16[8,128,1536]{2,1,0:T(8,128)(2,1)} %get-tuple-element.294), channel_id=1, source_target_pairs={{2,0},{3,1},{4,2},{5,3},{6,4},{7,5},{10,8},{11,9},{12,10},{13,11},... | collective-permute-start | bytes 9437192 | tf_op jit(solution)/shard_map/ppermute | solution.py:17
  1045.0 152.4 %copy-start.40 = (bf16[8,128,768]{2,1,0:T(8,128)(2,1)S(1)}, bf16[8,128,768]{2,1,0:T(8,128)(2,1)}, u32[]{:S(2)}) copy-start(bf16[8,128,768]{2,1,0:T(8,128)(2,1)} %param.22) | copy-start | bytes 4718596
  1045.0 389.8 %reduce-scatter.23.cloned.1.call-start = ((), (), s32[]{:S(2)}) async-start(), calls=%async_computation.17 | async-start | bytes 2433024
  1203.9 335.3 %reduce-scatter.21.cloned.1.call-start = ((), (), s32[]{:S(2)}) async-start(), calls=%async_computation.16 | async-start | bytes 2433024
  1207.3 473.6 %reduce-scatter.15.cloned.1.call-start = ((), (), s32[]{:S(2)}) async-start(), calls=%async_computation.13 | async-start | bytes 9732096 | tf_op jit(solution)/shard_map/reduce_scatter | solution.py:330
  1218.1 604.3 %reduce-scatter.17.cloned.1.call-start = ((), (), s32[]{:S(2)}) async-start(), calls=%async_computation.14 | async-start | bytes 9732096 | tf_op jit(solution)/shard_map/reduce_scatter | solution.py:332
  1232.0 5.1 copy-start.6
  1232.0 5.3 copy-start.31
  1232.0 5.4 copy-start.32
  1232.0 5.4 copy-start.33
  1232.0 5.4 copy-start.34
  1232.0 5.4 copy-start.35
  1232.0 5.4 copy-start.38
  1232.0 5.4 copy-start.39
  (18 other events, 40.7 us)
Sparse Core Ops, SparseCore 0:
  10.9 56.9 all-gather.6
  70.8 53.1 all-gather.8
  127.0 284.4 all-gather.10
  414.2 100.2 all-gather.12
  517.3 62.3 all-gather.14
  582.5 61.8 all-gather.16
  965.1 260.7 reduce-scatter.12
  1231.7 98.5 reduce-scatter.18
  1336.2 98.6 reduce-scatter.22
  1440.6 98.5 reduce-scatter.20
  1545.7 135.2 reduce-scatter.14
  1687.2 135.1 reduce-scatter.16
where the time goes:
time: 1840 us; the launch traced here: 1830 us
  waiting for transfers between devices  1070 us (58%)
  matrix products  228 us (12%)
  local copies, waits for them, and re-layouts  226 us (12%)
  blocking collectives  150 us (8%)
  other arithmetic  100 us (5%)
  starting transfers between devices  40.3 us (2%)
    ppermute x12, waiting for transfers between devices, passed_along(): return lax.ppermute(block, axis, route)  299 us
    unnamed x15, waiting for transfers between devices  186 us
    unnamed x2, blocking collectives  150 us
    all_gather x1, waiting for transfers between devices, body(): lax.all_gather(shards[0], ('rows', 'seq'), axis=0, tiled=True)  148 us
    reduce_scatter x1, waiting for transfers between devices, body(): lax.psum_scatter(partial_grads[9], ('rows', 'seq'), scatter_dimension=0,...  142 us
    reduce_scatter x1, waiting for transfers between devices, body(): lax.psum_scatter(partial_grads[11], ('rows', 'seq'), scatter_dimension=0,...  141 us
    dynamic_update_slice x16, local copies, waits for them, and re-layouts, body(): lax.map(partial(attend_back, score_scale=score_scale), (query_b, window,...  92 us
    all_gather x1, waiting for transfers between devices, body(): lax.all_gather(shards[9], ('rows', 'seq'), axis=0, tiled=True)  60.8 us
  transfers between devices with their start and end apart: 24, of which 16 were waited for; matrix products, arithmetic and copies ran while one was open for 12% of the time, Pallas kernels for 0%

commit v1 on v0

--- a/solution.py
+++ b/solution.py
@@ -9,6 +9,18 @@
 REACH = 3
 epsilon = 1e-12
 masked_score = -1e30
+
+
+def gather_by_bits(x, axis, dim):
+    ways, here = (lax.axis_size(axis), lax.axis_index(axis))
+    grown, reach = (x, 1)
+    while reach < ways:
+        theirs = lax.ppermute(grown, axis, [(d, d ^ reach) for d in range(ways)])
+        mine_first = jnp.concatenate([grown, theirs], axis=dim)
+        theirs_first = jnp.concatenate([theirs, grown], axis=dim)
+        grown = jnp.where(here & reach == 0, mine_first, theirs_first)
+        reach = 2 * reach
+    return grown
 
 
 def passed_along(block, axis, distance):
@@ -169,7 +181,7 @@
         final_shift,
     )
     gathered = (
-        lax.all_gather(shards[0], ("rows", "seq"), axis=0, tiled=True),
+        gather_by_bits(shards[0], ("rows", "seq"), 0),
         lax.all_gather(shards[1], ("rows", "seq"), axis=0, tiled=True),
         lax.all_gather(shards[2], ("rows", "seq"), axis=0, tiled=True),
         lax.all_gather(shards[3], ("rows", "seq"), axis=0, tiled=True),

time: 1840 us -> 1900 us (1.033)
  starting transfers between devices: 40.3 us -> 253 us
  waiting for transfers between devices: 1070 us -> 927 us
    all_gather x1 -> x0, waiting for transfers between devices: 148 us -> none  [body(): lax.all_gather(shards[0], ('rows', 'seq'), axis=0, tiled=True)]
    ppermute x12, starting transfers between devices: 39.7 us -> 181 us  [passed_along(): return lax.ppermute(block, axis, route)]
    ppermute x0 -> x5, starting transfers between devices: none -> 71.8 us  [gather_by_bits(): theirs = lax.ppermute(grown, axis, [(d, d ^ reach) for d in range(ways)])]
    all_gather x1, waiting for transfers between devices: 60.8 us -> 0.02 us  [body(): lax.all_gather(shards[9], ('rows', 'seq'), axis=0, tiled=True)]
    ppermute x12, waiting for transfers between devices: 299 us -> 331 us  [passed_along(): return lax.ppermute(block, axis, route)]
    all_gather x1, waiting for transfers between devices: 28.9 us -> 48 us  [body(): lax.all_gather(shards[11], ('rows', 'seq'), axis=0, tiled=True)]
    unnamed x15 -> x14, waiting for transfers between devices: 186 us -> 184 us
    unnamed x123 -> x129, local copies, waits for them, and re-layouts: 53.7 us -> 53.7 us
  transfers between devices with their start and end apart: 24 -> 28, of which waited for: 16 -> 18; matrix products, arithmetic and copies ran while one was open for 12% -> 12% of each run, Pallas kernels for 0% -> 0%
where the time goes in v1:
time: 1900 us; the launch traced here: 1890 us
  waiting for transfers between devices  927 us (49%)
  starting transfers between devices  253 us (13%)
  matrix products  228 us (12%)
  local copies, waits for them, and re-layouts  224 us (12%)
  blocking collectives  136 us (7%)
  other arithmetic  100 us (5%)
    ppermute x12, waiting for transfers between devices, passed_along(): return lax.ppermute(block, axis, route)  331 us
    unnamed x14, waiting for transfers between devices  184 us
    ppermute x12, starting transfers between devices, passed_along(): return lax.ppermute(block, axis, route)  181 us
    reduce_scatter x1, waiting for transfers between devices, body(): lax.psum_scatter(partial_grads[11], ('rows', 'seq'), scatter_dimension=0,...  142 us
    reduce_scatter x1, waiting for transfers between devices, body(): lax.psum_scatter(partial_grads[9], ('rows', 'seq'), scatter_dimension=0,...  142 us
    unnamed x2, blocking collectives  136 us
    dynamic_update_slice x16, local copies, waits for them, and re-layouts, body(): lax.map(partial(attend_back, score_scale=score_scale), (query_b, window,...  92.4 us
    ppermute x5, starting transfers between devices, gather_by_bits(): theirs = lax.ppermute(grown, axis, [(d, d ^ reach) for d in range(ways)])  71.8 us
  transfers between devices with their start and end apart: 28, of which 18 were waited for; matrix products, arithmetic and copies ran while one was open for 12% of the time, Pallas kernels for 0%

profile of v1, /device:TPU:0, one launch (start us, length us, event | category | flops | bytes accessed | tf_op | source)
XLA Modules:
  0.0 1886.1 jit_solution(2946182522844458332)
XLA Ops:
  17.6 42.6 %all-reduce.20 = (bf16[768]{0:T(1024)(128)(2,1)S(1)}, bf16[768]{0:T(1024)(128)(2,1)S(1)}, bf16[768]{0:T(1024)(128)(2,1)S(1)}, bf16[768]{0:T(1024)(128)(2,1)S(1)}...) all-reduce(bf16[768]{0:T(1024)(128)(2,1)S(1)} %dynamic-update-slice, ...), channel_id=1, replica_groups=mesh['rows'=4,'seq'=8] {'rows','seq'}, use_global_device_ids=true, to_apply=%add.3 | all-reduce | flops 9216 | bytes 36864
  60.2 7.8 all-gather.6.cloned.1.call-done
  69.3 54.6 %all-gather.8.cloned.1.call-done = bf16[768,768]{1,0:T(8,128)(2,1)} async-done(((bf16[24,768]{1,0:T(8,128)(2,1)}), bf16[768,768]{1,0:T(8,128)(2,1)}) %all-gather.8.cloned.1.call-update) | async-done | bytes 1179664 | tf_op jit(solution)/shard_map/all_gather | solution.py:187
  141.9 65.6 %collective-permute-start.7 = (bf16[48,768]{1,0:T(8,128)(2,1)S(1)}, bf16[48,768]{1,0:T(8,128)(2,1)S(1)}, u32[]{:S(2)}, u32[]{:S(2)}) collective-permute-start(bf16[48,768]{1,0:T(8,128)(2,1)S(1)} %maximum_select_fusion.6), channel_id=1, source_target_pairs={{0,2},{1,3},{2,0},{3,1},{4,6},{5,7},{6,4},{7,5},{8,10},{9,11},{10,... | collective-permute-start | bytes 221192 | tf_op jit(solution)/shard_map/ppermute | solution.py:18
  221.6 69.8 %collective-permute-start.2 = (bf16[8,128,1536]{1,2,0:T(8,128)(2,1)}, bf16[8,128,1536]{1,2,0:T(8,128)(2,1)}, u32[]{:S(2)}, u32[]{:S(2)}) collective-permute-start(bf16[8,128,1536]{1,2,0:T(8,128)(2,1)} %copy.92), channel_id=1, source_target_pairs={{0,1},{1,2},{2,3},{3,4},{4,5},{5,6},{6,7},{8,9},{9,10},{10,11},{11... | collective-permute-start | bytes 9437192 | tf_op jit(solution)/shard_map/ppermute | solution.py:29
  297.4 10.9 collective-permute-done.10
  322.7 116.4 %collective-permute-done.2 = bf16[8,128,1536]{1,2,0:T(8,128)(2,1)} collective-permute-done((bf16[8,128,1536]{1,2,0:T(8,128)(2,1)}, bf16[8,128,1536]{1,2,0:T(8,128)(2,1)}, u32[]{:S(2)}, u32[]{:S(2)}) %collective-permute-start.2) | collective-permute-done | bytes 3145760 | tf_op jit(solution)/shard_map/ppermute | solution.py:29
  447.1 8.0 collective-permute-done.4
  457.8 11.1 collective-permute-done.5
  471.5 7.3 copy-done
  478.8 64.9 %while.24 = (s32[]{:T(128)}, bf16[8,128,12,64]{1,3,2,0:T(8,128)(2,1)}, f32[8,12,128]{2,1,0:T(8,128)}, bf16[8,896,1536]{1,2,0:T(8,128)(2,1)}, pred[8,128,896]{2,1...) while((s32[]{:T(128)}, bf16[8,128,12,64]{1,3,2,0:T(8,128)(2,1)}, ...), condition=%wide.region_6.7_spmd, body=%wide.region_3.6_spmd.sunk | while | flops 368933376 | bytes 31295592 | solution.py:242
  552.9 36.4 %multiply_convert_fusion.1 = (bf16[1024,3072]{1,0:T(8,128)(2,1)}, f32[1024,3072]{1,0:T(8,128)}, f32[1024,3072]{1,0:T(8,128)}) fusion(f32[3072]{0:T(1024)S(1)} %convert_element_type.164, bf16[768,3072]{1,0:T(8,128)(2,1)} %all-gather.12.cloned.1.call-done, f32[1024,768]{1,0:T(8,128)S(1)} %get-tuple-element.300, f32[768]{0:T(1024)S(1)} %convert_element_type.162, ...), kind=kOutput, calls=%fused_computation.56 | convolution fusion | flops 5043388416 | bytes 39348224 | tf_op jit(solution)/shard_map/dot_general | solution.py:253
  589.2 48.0 %all-gather.14.cloned.1.call-done = bf16[3072,768]{1,0:T(8,128)(2,1)} async-done(((bf16[96,768]{1,0:T(8,128)(2,1)}), bf16[3072,768]{1,0:T(8,128)(2,1)}) %all-gather.14.cloned.1.call-update) | async-done | bytes 4718608 | tf_op jit(solution)/shard_map/all_gather | solution.py:195
  637.2 9.0 fusion.78
  653.4 19.2 %convert_reduce_fusion = (f32[3072]{0:T(1024)}, bf16[1024,3072]{1,0:T(8,128)(2,1)}) fusion(f32[1024,3072]{1,0:T(8,128)} %get-tuple-element.280, bf16[3072,768]{1,0:T(8,128)(2,1)} %all-gather.14.cloned.1.call-done, f32[1024,768]{1,0:T(8,128)} %get-tuple-element.276, f32[1024,3072]{1,0:T(8,128)} %get-tuple-element.301, f32[3072]{0:T(1024)S(1)} %convert_element_type.164), kind=kOutput, calls=%fused_computation.54 | convolution fusion | flops 4886098944 | bytes 39346176 | tf_op jit(solution)/shard_map/td,fd->tf/dot_general | solution.py:275
  672.7 10.6 multiply_reduce_fusion.1
  690.4 225.9 %while.25 = (s32[]{:T(128)}, bf16[8,128,12,64]{1,3,2,0:T(8,128)(2,1)S(1)}, f32[8,896,1536]{2,1,0:T(8,128)}, bf16[8,896,1536]{1,2,0:T(8,128)(2,1)}, pred[8,128,89...) while((s32[]{:T(128)}, ...), condition=%wide.region_18.19_spmd, body=%wide.region_16.18_spmd.sunk | while | flops 903608832 | bytes 96761984 | solution.py:296
  707.1 6.2 copy.160
  713.3 5.4 constant_dynamic-update-slice_fusion.11
  735.3 6.2 copy.160
  741.5 5.4 constant_dynamic-update-slice_fusion.11
  763.6 6.2 copy.160
  791.8 6.2 copy.160
  798.0 5.3 constant_dynamic-update-slice_fusion.11
  820.0 6.2 copy.160
  826.2 5.4 constant_dynamic-update-slice_fusion.11
  848.2 6.2 copy.160
  876.4 6.2 copy.160
  882.6 5.4 constant_dynamic-update-slice_fusion.11
  904.7 6.2 copy.160
  910.9 5.4 constant_dynamic-update-slice_fusion.11
  916.3 23.9 %convert.8 = bf16[8,896,1536]{2,1,0:T(8,128)(2,1)} convert(f32[8,896,1536]{2,1,0:T(8,128)} %get-tuple-element.96) | non-fusion elementwise | flops 11010048 | bytes 66060288 | tf_op jit(solution)/shard_map/convert.5
  940.2 13.6 fusion.75
  957.9 15.9 collective-permute-start.16
  976.8 76.5 %collective-permute-start.14 = (bf16[8,128,1536]{2,1,0:T(8,128)(2,1)}, bf16[8,128,1536]{2,1,0:T(8,128)(2,1)}, u32[]{:S(2)}, u32[]{:S(2)}) collective-permute-start(bf16[8,128,1536]{2,1,0:T(8,128)(2,1)} %get-tuple-element.292), channel_id=1, source_target_pairs={{0,1},{1,2},{2,3},{3,4},{4,5},{5,6},{6,7},{8,9},{9,10},{10,11},{11... | collective-permute-start | bytes 9437192 | tf_op jit(solution)/shard_map/ppermute | solution.py:29
  1063.5 44.3 %collective-permute-done.16 = bf16[8,128,1536]{2,1,0:T(8,128)(2,1)} collective-permute-done((bf16[8,128,1536]{2,1,0:T(8,128)(2,1)}, bf16[8,128,1536]{2,1,0:T(8,128)(2,1)}, u32[]{:S(2)}, u32[]{:S(2)}) %collective-permute-start.16) | collective-permute-done | bytes 3145760 | tf_op jit(solution)/shard_map/ppermute | solution.py:29
  1107.8 66.4 %collective-permute-done.15 = bf16[8,128,1536]{2,1,0:T(8,128)(2,1)} collective-permute-done((bf16[8,128,1536]{2,1,0:T(8,128)(2,1)}, bf16[8,128,1536]{2,1,0:T(8,128)(2,1)}, u32[]{:S(2)}, u32[]{:S(2)}) %collective-permute-start.15) | collective-permute-done | bytes 3145760 | tf_op jit(solution)/shard_map/ppermute | solution.py:29
  1174.2 79.7 %collective-permute-done.14 = bf16[8,128,1536]{2,1,0:T(8,128)(2,1)} collective-permute-done((bf16[8,128,1536]{2,1,0:T(8,128)(2,1)}, bf16[8,128,1536]{2,1,0:T(8,128)(2,1)}, u32[]{:S(2)}, u32[]{:S(2)}) %collective-permute-start.14) | collective-permute-done | bytes 3145760 | tf_op jit(solution)/shard_map/ppermute | solution.py:29
  1259.2 9.8 add_convert_fusion.1
  1279.0 10.7 fusion.68
  1291.6 10.2 fusion.65
  1303.6 5.4 fusion.46
  1309.4 93.7 %all-reduce.19 = (f32[768]{0:T(1024)S(1)}, f32[768]{0:T(1024)S(1)}, f32[768]{0:T(1024)S(1)}, f32[768]{0:T(1024)S(1)}, f32[768]{0:T(1024)S(1)}, /*index=5*/f32[30...) all-reduce(f32[768]{0:T(1024)S(1)} %reduce_sum.212, ...), channel_id=3, replica_groups=mesh['rows'=4,'seq'=8] {'rows','seq'}, use_global_device_ids=true, to_apply=%region_21.22.clone | all-reduce | flops 9216 | bytes 73728
  1408.4 6.7 add_add_fusion
  1415.1 76.7 %reduce-scatter.23.cloned.1.call-done = f32[24,768]{1,0:T(8,128)} async-done(((f32[768,768]{1,0:T(8,128)}), f32[24,768]{1,0:T(8,128)}) %reduce-scatter.23.cloned.1.call-update) | async-done | bytes 73744
  1491.8 104.4 %reduce-scatter.21.cloned.1.call-done = f32[24,768]{1,0:T(8,128)} async-done(((f32[768,768]{1,0:T(8,128)}), f32[24,768]{1,0:T(8,128)}) %reduce-scatter.21.cloned.1.call-update) | async-done | bytes 73744
  1596.2 141.5 %reduce-scatter.15.cloned.1.call-done = f32[24,3072]{1,0:T(8,128)} async-done(((f32[768,3072]{1,0:T(8,128)}), f32[24,3072]{1,0:T(8,128)}) %reduce-scatter.15.cloned.1.call-update) | async-done | bytes 294928 | tf_op jit(solution)/shard_map/reduce_scatter | solution.py:342
  1737.7 141.6 %reduce-scatter.17.cloned.1.call-done = f32[96,768]{1,0:T(8,128)} async-done(((f32[3072,768]{1,0:T(8,128)}), f32[96,768]{1,0:T(8,128)}) %reduce-scatter.17.cloned.1.call-update) | async-done | bytes 294928 | tf_op jit(solution)/shard_map/reduce_scatter | solution.py:344
  (387 shorter events, 349.8 us)
Async XLA Ops:
  7.2 60.8 %all-gather.6.cloned.1.call-start = ((), (), s32[]{:S(2)}) async-start(), calls=%async_computation.6 | async-start | bytes 1216512 | tf_op jit(solution)/shard_map/all_gather | solution.py:186
  7.9 116.0 %all-gather.8.cloned.1.call-start = ((), (), s32[]{:S(2)}) async-start(), calls=%async_computation.7 | async-start | bytes 1216512 | tf_op jit(solution)/shard_map/all_gather | solution.py:187
  8.7 539.7 %all-gather.10.cloned.1.call-start = ((), (), s32[]{:S(2)}) async-start(), calls=%async_computation.8 | async-start | bytes 1216512 | tf_op jit(solution)/shard_map/all_gather | solution.py:189
  9.4 543.4 %all-gather.12.cloned.1.call-start = ((), (), s32[]{:S(2)}) async-start(), calls=%async_computation.9 | async-start | bytes 4866048 | tf_op jit(solution)/shard_map/all_gather | solution.py:193
  10.0 627.3 %all-gather.14.cloned.1.call-start = ((), (), s32[]{:S(2)}) async-start(), calls=%async_computation.10 | async-start | bytes 4866048 | tf_op jit(solution)/shard_map/all_gather | solution.py:195
  131.5 6.4 copy-start.30
  131.5 83.4 %copy-start.38 = (s32[8,4]{0,1:T(4,128)S(1)}, s32[8,4]{0,1:T(4,128)}, u32[]{:S(2)}) copy-start(s32[8,4]{0,1:T(4,128)} %param.24) | copy-start | bytes 388
  134.3 175.9 %collective-permute-start = (bf16[8,128,1536]{1,2,0:T(8,128)(2,1)}, bf16[8,128,1536]{1,2,0:T(8,128)(2,1)S(1)}, u32[]{:S(2)}, u32[]{:S(2)}) collective-permute-start(bf16[8,128,1536]{1,2,0:T(8,128)(2,1)} %copy.92), channel_id=1, source_target_pairs={{0,3},{1,4},{2,5},{3,6},{4,7},{8,11},{9,12},{10,13},{11,14},{12,15... | collective-permute-start | bytes 9437192 | tf_op jit(solution)/shard_map/ppermute | solution.py:29
  137.9 4.0 collective-permute-start.6
  139.0 1276.0 %reduce-scatter.13.cloned.1.call-start = ((), (), s32[]{:S(2)}) async-start(), calls=%async_computation.11 | async-start | bytes 2433024 | tf_op jit(solution)/shard_map/reduce_scatter | solution.py:338
  141.9 68.0 %collective-permute-start.7 = (bf16[48,768]{1,0:T(8,128)(2,1)S(1)}, bf16[48,768]{1,0:T(8,128)(2,1)S(1)}, u32[]{:S(2)}, u32[]{:S(2)}) collective-permute-start(bf16[48,768]{1,0:T(8,128)(2,1)S(1)} %maximum_select_fusion.6), channel_id=1, source_target_pairs={{0,2},{1,3},{2,0},{3,1},{4,6},{5,7},{6,4},{7,5},{8,10},{9,11},{10,... | collective-permute-start | bytes 221192 | tf_op jit(solution)/shard_map/ppermute | solution.py:18
  209.9 11.5 collective-permute-start.8
  214.9 81.2 %copy-start.28 = (f32[768]{0:T(1024)}, f32[768]{0:T(1024)S(1)}, u32[]{:S(2)}) copy-start(f32[768]{0:T(1024)S(1)} %convert_element_type.167) | copy-start | bytes 9220
  215.0 105.1 %collective-permute-start.1 = (bf16[8,128,1536]{1,2,0:T(8,128)(2,1)}, bf16[8,128,1536]{1,2,0:T(8,128)(2,1)}, u32[]{:S(2)}, u32[]{:S(2)}) collective-permute-start(bf16[8,128,1536]{1,2,0:T(8,128)(2,1)} %copy.92), channel_id=1, source_target_pairs={{0,2},{1,3},{2,4},{3,5},{4,6},{5,7},{8,10},{9,11},{10,12},{11,13},... | collective-permute-start | bytes 9437192 | tf_op jit(solution)/shard_map/ppermute | solution.py:29
  221.4 70.0 %collective-permute-start.9 = (bf16[192,768]{1,0:T(8,128)(2,1)S(1)}, bf16[192,768]{1,0:T(8,128)(2,1)S(1)}, u32[]{:S(2)}, u32[]{:S(2)}) collective-permute-start(bf16[192,768]{1,0:T(8,128)(2,1)S(1)} %maximum_select_fusion.2), channel_id=1, source_target_pairs={{0,8},{1,9},{2,10},{3,11},{4,12},{5,13},{6,14},{7,15},{8,0},{9,1},... | collective-permute-start | bytes 884744 | tf_op jit(solution)/shard_map/ppermute | solution.py:18
  221.6 217.6 %collective-permute-start.2 = (bf16[8,128,1536]{1,2,0:T(8,128)(2,1)}, bf16[8,128,1536]{1,2,0:T(8,128)(2,1)}, u32[]{:S(2)}, u32[]{:S(2)}) collective-permute-start(bf16[8,128,1536]{1,2,0:T(8,128)(2,1)} %copy.92), channel_id=1, source_target_pairs={{0,1},{1,2},{2,3},{3,4},{4,5},{5,6},{6,7},{8,9},{9,10},{10,11},{11... | collective-permute-start | bytes 9437192 | tf_op jit(solution)/shard_map/ppermute | solution.py:29
  291.6 18.6 copy-start.19
  291.6 16.7 collective-permute-start.10
  296.1 148.4 %collective-permute-start.3 = (bf16[8,128,1536]{1,2,0:T(8,128)(2,1)}, bf16[8,128,1536]{1,2,0:T(8,128)(2,1)}, u32[]{:S(2)}, u32[]{:S(2)}) collective-permute-start(bf16[8,128,1536]{1,2,0:T(8,128)(2,1)} %copy.92), channel_id=1, source_target_pairs={{1,0},{2,1},{3,2},{4,3},{5,4},{6,5},{7,6},{9,8},{10,9},{11,10},{12... | collective-permute-start | bytes 9437192 | tf_op jit(solution)/shard_map/ppermute | solution.py:29
  308.3 146.8 %collective-permute-start.4 = (bf16[8,128,1536]{1,2,0:T(8,128)(2,1)}, bf16[8,128,1536]{1,2,0:T(8,128)(2,1)}, u32[]{:S(2)}, u32[]{:S(2)}) collective-permute-start(bf16[8,128,1536]{1,2,0:T(8,128)(2,1)} %copy.92), channel_id=1, source_target_pairs={{2,0},{3,1},{4,2},{5,3},{6,4},{7,5},{10,8},{11,9},{12,10},{13,11},... | collective-permute-start | bytes 9437192 | tf_op jit(solution)/shard_map/ppermute | solution.py:29
  310.2 158.6 %collective-permute-start.5 = (bf16[8,128,1536]{1,2,0:T(8,128)(2,1)}, bf16[8,128,1536]{1,2,0:T(8,128)(2,1)}, u32[]{:S(2)}, u32[]{:S(2)}) collective-permute-start(bf16[8,128,1536]{1,2,0:T(8,128)(2,1)} %copy.92), channel_id=1, source_target_pairs={{3,0},{4,1},{5,2},{6,3},{7,4},{11,8},{12,9},{13,10},{14,11},{15,12... | collective-permute-start | bytes 9437192 | tf_op jit(solution)/shard_map/ppermute | solution.py:29
  311.9 371.3 %copy-start.24 = (f32[768]{0:T(1024)}, f32[768]{0:T(1024)S(1)}, u32[]{:S(2)}) copy-start(f32[768]{0:T(1024)S(1)} %convert_element_type.161) | copy-start | bytes 9220
  311.9 325.3 %copy-start.26 = (f32[768]{0:T(1024)}, f32[768]{0:T(1024)S(1)}, u32[]{:S(2)}) copy-start(f32[768]{0:T(1024)S(1)} %convert_element_type.162) | copy-start | bytes 9220
  471.5 7.3 copy-start
  552.3 131.0 %copy-start.1 = (f32[1024,768]{1,0:T(8,128)}, f32[1024,768]{1,0:T(8,128)S(1)}, u32[]{:S(2)}) copy-start(f32[1024,768]{1,0:T(8,128)S(1)} %get-tuple-element.300) | copy-start | bytes 9437188
  552.3 131.0 %copy-start.20 = (f32[1024]{0:T(1024)}, f32[1024]{0:T(1024)S(1)}, u32[]{:S(2)}) copy-start(f32[1024]{0:T(1024)S(1)} %broadcast_multiply_fusion.4) | copy-start | bytes 12292
  552.8 130.5 %copy-start.22 = (f32[1024]{0:T(1024)}, f32[1024]{0:T(1024)S(1)}, u32[]{:S(2)}) copy-start(f32[1024]{0:T(1024)S(1)} %add_rsqrt_fusion.1) | copy-start | bytes 12292
  552.8 84.4 %copy-start.39 = (f32[768]{0:T(1024)S(1)}, f32[768]{0:T(1024)}, u32[]{:S(2)}) copy-start(f32[768]{0:T(1024)} %convert_element_type.166) | copy-start | bytes 9220
  916.3 140.0 %copy-start.8 = (bf16[8,128,12,64]{1,3,2,0:T(8,128)(2,1)}, bf16[8,128,12,64]{1,3,2,0:T(8,128)(2,1)S(1)}, u32[]{:S(2)}) copy-start(bf16[8,128,12,64]{1,3,2,0:T(8,128)(2,1)S(1)} %get-tuple-element.95) | copy-start | bytes 4718596
  940.2 14.9 copy-start.14
  940.2 14.9 copy-start.16
  953.8 101.2 %collective-permute-start.11 = (bf16[8,128,1536]{2,1,0:T(8,128)(2,1)}, bf16[8,128,1536]{2,1,0:T(8,128)(2,1)}, u32[]{:S(2)}, u32[]{:S(2)}) collective-permute-start(bf16[8,128,1536]{2,1,0:T(8,128)(2,1)} %get-tuple-element.289), channel_id=1, source_target_pairs={{3,0},{4,1},{5,2},{6,3},{7,4},{11,8},{12,9},{13,10},{14,11},{15,12... | collective-permute-start | bytes 9437192 | tf_op jit(solution)/shard_map/ppermute | solution.py:29
  957.9 457.2 %reduce-scatter.19.cloned.1.call-start = ((), (), s32[]{:S(2)}) async-start(), calls=%async_computation.14 | async-start | bytes 2433024
  957.9 149.9 %collective-permute-start.16 = (bf16[8,128,1536]{2,1,0:T(8,128)(2,1)}, bf16[8,128,1536]{2,1,0:T(8,128)(2,1)}, u32[]{:S(2)}, u32[]{:S(2)}) collective-permute-start(bf16[8,128,1536]{2,1,0:T(8,128)(2,1)} %get-tuple-element.290), channel_id=1, source_target_pairs={{0,3},{1,4},{2,5},{3,6},{4,7},{8,11},{9,12},{10,13},{11,14},{12,15... | collective-permute-start | bytes 9437192 | tf_op jit(solution)/shard_map/ppermute | solution.py:29
  973.8 200.4 %collective-permute-start.15 = (bf16[8,128,1536]{2,1,0:T(8,128)(2,1)}, bf16[8,128,1536]{2,1,0:T(8,128)(2,1)}, u32[]{:S(2)}, u32[]{:S(2)}) collective-permute-start(bf16[8,128,1536]{2,1,0:T(8,128)(2,1)} %get-tuple-element.291), channel_id=1, source_target_pairs={{0,2},{1,3},{2,4},{3,5},{4,6},{5,7},{8,10},{9,11},{10,12},{11,13},... | collective-permute-start | bytes 9437192 | tf_op jit(solution)/shard_map/ppermute | solution.py:29
  976.8 277.2 %collective-permute-start.14 = (bf16[8,128,1536]{2,1,0:T(8,128)(2,1)}, bf16[8,128,1536]{2,1,0:T(8,128)(2,1)}, u32[]{:S(2)}, u32[]{:S(2)}) collective-permute-start(bf16[8,128,1536]{2,1,0:T(8,128)(2,1)} %get-tuple-element.292), channel_id=1, source_target_pairs={{0,1},{1,2},{2,3},{3,4},{4,5},{5,6},{6,7},{8,9},{9,10},{10,11},{11... | collective-permute-start | bytes 9437192 | tf_op jit(solution)/shard_map/ppermute | solution.py:29
  1053.3 200.7 %collective-permute-start.13 = (bf16[8,128,1536]{2,1,0:T(8,128)(2,1)}, bf16[8,128,1536]{2,1,0:T(8,128)(2,1)}, u32[]{:S(2)}, u32[]{:S(2)}) collective-permute-start(bf16[8,128,1536]{2,1,0:T(8,128)(2,1)} %get-tuple-element.293), channel_id=1, source_target_pairs={{1,0},{2,1},{3,2},{4,3},{5,4},{6,5},{7,6},{9,8},{10,9},{11,10},{12... | collective-permute-start | bytes 9437192 | tf_op jit(solution)/shard_map/ppermute | solution.py:29
  1055.0 204.3 %collective-permute-start.12 = (bf16[8,128,1536]{2,1,0:T(8,128)(2,1)}, bf16[8,128,1536]{2,1,0:T(8,128)(2,1)}, u32[]{:S(2)}, u32[]{:S(2)}) collective-permute-start(bf16[8,128,1536]{2,1,0:T(8,128)(2,1)} %get-tuple-element.294), channel_id=1, source_target_pairs={{2,0},{3,1},{4,2},{5,3},{6,4},{7,5},{10,8},{11,9},{12,10},{13,11},... | collective-permute-start | bytes 9437192 | tf_op jit(solution)/shard_map/ppermute | solution.py:29
  1063.5 205.6 %copy-start.42 = (bf16[8,128,768]{2,1,0:T(8,128)(2,1)S(1)}, bf16[8,128,768]{2,1,0:T(8,128)(2,1)}, u32[]{:S(2)}) copy-start(bf16[8,128,768]{2,1,0:T(8,128)(2,1)} %param.22) | copy-start | bytes 4718596
  1063.5 428.3 %reduce-scatter.23.cloned.1.call-start = ((), (), s32[]{:S(2)}) async-start(), calls=%async_computation.16 | async-start | bytes 2433024
  1275.5 320.7 %reduce-scatter.21.cloned.1.call-start = ((), (), s32[]{:S(2)}) async-start(), calls=%async_computation.15 | async-start | bytes 2433024
  1278.9 458.9 %reduce-scatter.15.cloned.1.call-start = ((), (), s32[]{:S(2)}) async-start(), calls=%async_computation.12 | async-start | bytes 9732096 | tf_op jit(solution)/shard_map/reduce_scatter | solution.py:342
  1289.7 589.7 %reduce-scatter.17.cloned.1.call-start = ((), (), s32[]{:S(2)}) async-start(), calls=%async_computation.13 | async-start | bytes 9732096 | tf_op jit(solution)/shard_map/reduce_scatter | solution.py:344
  1303.6 5.8 copy-start.35
  1303.6 5.8 copy-start.36
  1303.6 5.8 copy-start.37
  1303.6 5.8 copy-start.40
  1303.6 5.8 copy-start.41
  (25 other events, 74.1 us)
Sparse Core Ops, SparseCore 0:
  10.9 57.0 all-gather.5
  70.9 53.0 all-gather.7
  126.9 180.0 all-gather.9
  309.7 209.6 all-gather.11
  522.1 115.0 all-gather.13
  958.0 324.5 reduce-scatter.12
  1288.5 98.6 reduce-scatter.18
  1393.1 98.6 reduce-scatter.22
  1497.6 98.5 reduce-scatter.20
  1602.5 135.1 reduce-scatter.14
  1744.2 135.1 reduce-scatter.16
